TPU v7x, 32 devices: a whole 2x2x4 slice. The times are simulated.
32 devices in a mesh: row: 8 (over z, x), col: 4 (over y, core).
Axes of the slice: x: 2, y: 2, z: 4, core: 2. Of those that a mesh axis runs over, the one named last changes fastest.
Arguments:
- factor: float32 [9, 1024, 3, 512], P(None, 'row', None, 'col'), may hold values from -2 to 2.5, as said below
- adjoint: float32 [9, 1024, 3, 512], P(None, 'row', None, 'col'), may hold values from -6 to 6
Outputs:
- kernel_adjoint: float32 [9, 1024, 3, 512], P(None, 'row', None, 'col')
Inputs may be any that keep to these rules, and one draw needn't show every extreme that they name: `factor`: zero where the column minus 512 exceeds the row; the diagonal entries of the two 512-square diagonal blocks lie between 1 and 2.5.
All inputs are finite; a program needn't handle non-finite values.
Results may differ from a plain program's by a relative error of at most 0.0001.
Values sent between devices are 32-bit elements; how exact they have to be, the bound alone decides.
A program may use at most 64 MiB of HBM per device.

v0:
```python
import jax
import jax.numpy as jnp
from jax import lax
from jax.sharding import PartitionSpec as P

NB = 512


def exact_dot(first, second):
    return jnp.dot(
        first, second, precision=lax.Precision.HIGHEST, preferred_element_type=jnp.float32
    )


def lower_half(matrix):
    return jnp.tril(matrix) - 0.5 * jnp.diag(jnp.diag(matrix))


def local(factor, adjoint):
    row_cycles, tile_rows, col_cycles, tile_cols = factor.shape
    col_devices = lax.axis_size("col")
    row_devices = lax.axis_size("row")
    row_span = tile_rows * row_devices
    col_span = tile_cols * col_devices
    row_index = lax.axis_index("row")
    col_index = lax.axis_index("col")
    local_rows = row_cycles * tile_rows
    local_cols = col_cycles * tile_cols
    left_cols = col_cycles * col_span - 2 * NB
    panel_cycles = 2 * NB // col_span
    row_blocks = 2 * NB // row_span
    owned_rows = row_blocks * tile_rows
    owned_cols = panel_cycles * tile_cols
    split_col = local_cols - owned_cols
    row_steps = jnp.arange(local_rows, dtype=jnp.int32)
    col_steps = jnp.arange(local_cols, dtype=jnp.int32)
    global_rows = row_steps // tile_rows * row_span + row_index * tile_rows + row_steps % tile_rows
    global_cols = col_steps // tile_cols * col_span + col_index * tile_cols + col_steps % tile_cols
    factor_flat = factor.reshape(local_rows, local_cols)
    working = jnp.where(
        global_cols[None, :] - left_cols > global_rows[:, None],
        0.0,
        adjoint.reshape(local_rows, local_cols),
    )
    factor_local = factor_flat[:, split_col:].reshape(local_rows, panel_cycles, tile_cols)
    factor_panels = lax.all_gather(factor_local, "col", axis=2, tiled=True).reshape(
        local_rows, 2 * NB
    )
    factor_tops = factor_flat[:owned_rows].reshape(row_blocks, tile_rows, local_cols)
    diag_part = factor_panels[:owned_rows].reshape(row_blocks, tile_rows, 2 * NB)
    top_rows, diag_full = (
        lax.all_gather(factor_tops, "row", axis=1, tiled=True),
        lax.all_gather(diag_part, "row", axis=1, tiled=True),
    )
    top_rows = top_rows.reshape(2 * NB, local_cols)
    diag_full = diag_full.reshape(2 * NB, 2 * NB)
    owned_global = global_rows[:owned_rows]
    block_ids = jnp.arange(NB, dtype=jnp.int32)
    panel_globals = global_cols[split_col:]
    first_row = NB
    bottom = first_row + NB
    first_col = left_cols + first_row
    beneath = (global_rows >= bottom)[:, None]
    col_left = (global_cols < first_col)[None, :]
    adjoint_local = working[:, split_col:].reshape(local_rows, panel_cycles, tile_cols)
    adjoint_panels = lax.all_gather(adjoint_local, "col", axis=2, tiled=True).reshape(
        local_rows, 2 * NB
    )
    diag_block = diag_full[first_row:bottom, first_row:bottom]
    panel_factor = jnp.where(beneath, factor_panels[:, first_row:bottom], 0.0)
    solved_cols = lax.linalg.triangular_solve(
        diag_block, adjoint_panels[:, first_row:bottom], left_side=False, lower=True
    )
    column_adjoint = jnp.where(beneath, solved_cols, 0.0)
    picker = (owned_global[None, :] == first_row + block_ids[:, None]).astype(jnp.float32)
    partial_sum = exact_dot(picker, adjoint_panels[:owned_rows, first_row:bottom]) - jnp.tril(
        exact_dot(column_adjoint.T, panel_factor)
    )
    diag_start = lax.psum(partial_sum, "row")
    product = lower_half(exact_dot(diag_block.T, diag_start))
    left_solved = lax.linalg.triangular_solve(
        diag_block, product, left_side=True, lower=True, transpose_a=True
    )
    symmetric = lax.linalg.triangular_solve(diag_block, left_solved, left_side=False, lower=True)
    diag_adjoint = lower_half(symmetric + symmetric.T)
    owned_sym = exact_dot(picker.T, diag_adjoint + diag_adjoint.T)
    panel_rows_l = top_rows[first_row:bottom]
    trail_update = exact_dot(column_adjoint, panel_rows_l)
    row_extra = exact_dot(owned_sym, panel_rows_l)
    trail_factor = jnp.where(beneath & col_left, factor_flat, 0.0)
    row_terms = jnp.pad(
        exact_dot(column_adjoint.T, trail_factor), ((first_row, NB - first_row), (0, 0))
    ).reshape(row_blocks, row_span, local_cols)
    summed = lax.psum_scatter(row_terms, "row", scatter_dimension=1, tiled=True).reshape(
        owned_rows, local_cols
    )
    in_panel = ((owned_global >= first_row) & (owned_global < bottom))[:, None]
    row_change = jnp.where(in_panel & col_left, summed + row_extra, 0.0)
    working = working - jnp.where(beneath & col_left, trail_update, 0.0)
    working = jnp.concatenate([working[:owned_rows] - row_change, working[owned_rows:]], 0)
    owned_diag = exact_dot(picker.T, diag_adjoint)
    new_slot = jnp.where(beneath, column_adjoint, adjoint_panels[:, first_row:bottom])
    new_slot = jnp.concatenate(
        [jnp.where(in_panel, owned_diag, new_slot[:owned_rows]), new_slot[owned_rows:]], 0
    )
    new_panels = jnp.concatenate(
        [adjoint_panels[:, :first_row], new_slot, adjoint_panels[:, bottom:]], 1
    )
    local_new = lax.dynamic_index_in_dim(
        new_panels.reshape(local_rows, panel_cycles, col_devices, tile_cols),
        col_index,
        2,
        keepdims=False,
    ).reshape(local_rows, owned_cols)
    in_cols = ((panel_globals >= first_col) & (panel_globals < first_col + NB))[None, :]
    working = jnp.concatenate(
        [working[:, :split_col], jnp.where(in_cols, local_new, working[:, split_col:])], 1
    )
    return working.reshape(row_cycles, tile_rows, col_cycles, tile_cols)


def solution(mesh):
    in_specs = (P(None, "row", None, "col"), P(None, "row", None, "col"))
    out_specs = P(None, "row", None, "col")
    return jax.shard_map(local, mesh=mesh, in_specs=in_specs, out_specs=out_specs, check_vma=False)
```

profile of v0, /device:TPU:0, one launch (start us, length us, event | category | flops | bytes accessed | tf_op | source)
XLA Modules:
  0.0 376.3 jit_solution(3976893358861151109)
XLA Ops:
  6.5 2.7 copy.19
  9.4 1.2 copy-done.4
  10.7 1.4 copy.35
  12.2 40.3 %all-gather.7.cloned.1.call-done = f32[1152,2,512]{0,2,1:T(8,128)} async-done(((f32[1152,2,128]{0,2,1:T(8,128)}), f32[1152,2,512]{0,2,1:T(8,128)}) %all-gather.7.cloned.1.call-update) | async-done | bytes 4718608 | tf_op jit(solution)/shard_map/all_gather | solution.py:46
  52.5 1.9 slice.166
  54.4 1.2 copy.17
  55.9 1.2 copy-done.3
  57.2 1.4 copy.34
  60.3 68.9 %all-gather.9.cloned.1.call-done = f32[1,1024,1024]{1,2,0:T(8,128)} async-done(((f32[1,128,1024]{1,2,0:T(8,128)}), f32[1,1024,1024]{1,2,0:T(8,128)}) %all-gather.9.cloned.1.call-update) | async-done | bytes 4194320 | tf_op jit(solution)/shard_map/all_gather | solution.py:53
  129.2 1.3 fusion.19
  130.5 8.9 %while.1 = (s32[]{:T(128)}, f32[512,512]{0,1:T(8,128)S(1)}, s32[4,2]{0,1:T(2,128)S(1)}, f32[4,128,128]{2,1,0:T(8,128)S(1)}, s32[]{:T(128)}) while((s32[]{:T(128)}, f32[512,512]{0,1:T(8,128)S(1)}, s32[4,2]{0,1:T(2,128)S(1)}, f32[4,128,128]{2,1,0:T(8,128)S(1)}, s32[]{:T(128)}) %tuple.22), condition=%wide.while_cond, body=%wide.while_body.sunk | while | flops 2 | bytes 393329 | solution.py:71
  131.2 1.4 dynamic-slice.7
  133.4 1.4 dynamic-slice.7
  135.6 1.4 dynamic-slice.7
  137.8 1.4 dynamic-slice.7
  139.4 39.8 %custom-call.7 = f32[4,128,128]{1,2,0:T(8,128)S(1)} custom-call(f32[4,128,128]{2,1,0:T(8,128)S(1)} %get-tuple-element.12), custom_call_target="InvertDiagBlocksLowerTriangular" | custom-call | tf_op jit(solution)/shard_map/triangular_solve | solution.py:71
  179.3 1.9 fusion.34
  181.2 1.7 convolution_subtract_fusion.2
  183.6 2.0 convolution_subtract_fusion.1
  186.2 2.5 convolution_subtract_fusion
  188.7 1.5 fusion.69
  190.2 4.4 %fusion.9 = f32[512,512]{0,1:T(8,128)S(1)} fusion(f32[1152,1024]{0,1:T(8,128)S(1)} %bitcast.101, pred[1152]{0:T(1024)(128)(4,1)S(1)} %broadcast_compare_fusion, f32[1152,128]{0,1:T(8,128)S(1)} %fusion.34, f32[1152,128]{0,1:T(8,128)S(1)} %fusion.63, f32[1152,128]{0,1:T(8,128)S(1)} %fusion.66, f32[1152,128]{0,1:T(8,128)S(1)} %fusion.69), kind=kOutput, calls=%fused_computation.29 | convolution fusion | flops 3627352064 | bytes 5771264 | tf_op jit(solution)/shard_map/dot_general | solution.py:10
  194.6 2.7 convolution_subtract_fusion.3
  197.6 4.4 %fusion.102 = (f32[1152,512]{0,1:T(8,128)}, f32[1152,512]{0,1:T(8,128)S(1)}) fusion(f32[1152,1024]{0,1:T(8,128)} %bitcast.86, f32[1152,128]{0,1:T(8,128)S(1)} %fusion.34, f32[1152,128]{0,1:T(8,128)S(1)} %fusion.63, f32[1152,128]{0,1:T(8,128)S(1)} %fusion.66, f32[1152,128]{0,1:T(8,128)S(1)} %fusion.69, pred[1152]{0:T(1024)(128)(4,1)S(1)} %broadcast_compare_fusion), kind=kLoop, calls=%fused_computation.162 | loop fusion | flops 2949120 | bytes 11797632 | tf_op jit(solution)/shard_map/slice | solution.py:107
  202.0 1.5 copy-done.1
  203.5 1.6 slice.177
  205.1 7.7 %all-gather.11.cloned.1.call-done = f32[1,1024,384]{1,2,0:T(8,128)} async-done(((f32[1,128,384]{1,2,0:T(8,128)}), f32[1,1024,384]{1,2,0:T(8,128)}) %all-gather.11.cloned.1.call-update) | async-done | bytes 1572880 | tf_op jit(solution)/shard_map/all_gather | solution.py:52
  212.8 9.6 %fusion = f32[1152,384]{1,0:T(8,128)S(1)} fusion(f32[1152,384]{1,0:T(8,128)} %copy-done.3, pred[384]{0:T(512)(128)(4,1)S(1)} %broadcast_compare_fusion.1, pred[1152]{0:T(1024)(128)(4,1)S(1)} %broadcast_compare_fusion, f32[1,1024,384]{1,2,0:T(8,128)} %all-gather.11.cloned.1.call-done, f32[1152,128]{0,1:T(8,128)S(1)} %fusion.34, f32[1152,128]{0,1:T(8,128)S(1)} %fusion.63, ...), kind=kOutput, calls=%fused_computation.6 | convolution fusion | flops 2721595392 | bytes 6689280 | tf_op jit(solution)/shard_map/dot_general | solution.py:10
  222.4 1.2 slice.173
  223.6 1.4 copy-done.5
  225.1 4.7 %fusion.2 = f32[512,384]{1,0:T(8,128)S(1)} fusion(f32[1152,384]{1,0:T(8,128)S(1)} %bitcast.91, pred[384]{0:T(512)(128)(4,1)S(1)} %broadcast_compare_fusion.1, pred[1152]{0:T(1024)(128)(4,1)S(1)} %broadcast_compare_fusion, f32[1152,128]{0,1:T(8,128)S(1)} %fusion.34, f32[1152,128]{0,1:T(8,128)S(1)} %fusion.63, f32[1152,128]{0,1:T(8,128)S(1)} %fusion.66, ...), kind=kOutput, calls=%fused_computation.15 | convolution fusion | flops 2721153024 | bytes 4916736 | tf_op jit(solution)/shard_map/dot_general | solution.py:10
  229.8 1.3 pad_bitcast_fusion
  231.1 61.6 %all-reduce.3.cloned.1.call-done = f32[512,512]{0,1:T(8,128)} async-done(((f32[512,512]{0,1:T(8,128)}), f32[512,512]{0,1:T(8,128)}) %all-reduce.3.cloned.1.call-update) | async-done | bytes 1048592 | tf_op jit(solution)/shard_map/psum | solution.py:79
  292.7 3.4 convolution_bitcast_fusion
  296.1 4.5 %gather_fusion = f32[512]{0:T(512)S(1)} fusion(f32[512,512]{0,1:T(8,128)S(1)} %convolution_bitcast_fusion, s32[512]{0:T(512)S(1)} %bitcast.79), kind=kCustom, calls=%fused_computation | custom fusion | bytes 8192 | tf_op jit(solution)/shard_map/jit(_diag)/jit(diagonal)/cond/branch_0_fun/gather | solution.py:16
  303.6 1.5 convolution_subtract_fusion.9
  310.2 1.5 convolution_subtract_fusion.8
  312.1 1.1 pad_maximum_fusion.2
  314.7 4.8 %gather_fusion.1 = f32[512]{0:T(512)S(1)} fusion(f32[512,512]{0,1:T(8,128)S(1)} %bitcast_add_fusion.2, s32[512]{0:T(512)S(1)} %bitcast.80), kind=kCustom, calls=%fused_computation.1 | custom fusion | bytes 8192 | tf_op jit(solution)/shard_map/jit(_diag)/jit(diagonal)/cond/branch_0_fun/gather | solution.py:16
  319.6 1.3 copy.28
  321.0 1.6 convolution_select_fusion.1
  322.6 1.9 maximum_maximum_fusion
  325.0 2.1 fusion.18
  327.1 34.3 %reduce-scatter.2.cloned.1.call-done = f32[1,128,384]{2,1,0:T(8,128)} async-done(((f32[1,1024,384]{2,1,0:T(8,128)}), f32[1,128,384]{2,1,0:T(8,128)}) %reduce-scatter.2.cloned.1.call-update) | async-done | bytes 196624 | tf_op jit(solution)/shard_map/reduce_scatter | solution.py:94
  361.5 2.1 fusion.17
  363.7 1.3 fusion.3
  365.1 2.7 reshape.150
  367.7 1.4 copy.31
  (107 shorter events, 17.4 us)
Async XLA Ops:
  6.5 45.9 %all-gather.7.cloned.1.call-start = ((), (), s32[]{:S(2)}) async-start(), calls=%async_computation.2 | async-start | bytes 5898240 | tf_op jit(solution)/shard_map/all_gather | solution.py:46
  9.4 1.2 copy-start.4
  10.7 43.7 %copy-start.12 = (f32[9,128,3,128]{3,1,2,0:T(8,128)S(1)}, f32[9,128,3,128]{3,1,2,0:T(8,128)}, u32[]{:S(2)}) copy-start(f32[9,128,3,128]{3,1,2,0:T(8,128)} %param.3) | copy-start | bytes 5308420
  12.1 117.0 %all-gather.9.cloned.1.call-start = ((), (), s32[]{:S(2)}) async-start(), calls=%async_computation.3 | async-start | bytes 4718592 | tf_op jit(solution)/shard_map/all_gather | solution.py:53
  54.3 124.9 %all-gather.5.cloned.1.call-start = ((), (), s32[]{:S(2)}) async-start(), calls=%async_computation.1 | async-start | bytes 5898240 | tf_op jit(solution)/shard_map/all_gather | solution.py:66
  55.9 1.2 copy-start.3
  57.2 1.5 slice-start
  58.7 154.1 %all-gather.11.cloned.1.call-start = ((), (), s32[]{:S(2)}) async-start(), calls=%async_computation.4 | async-start | bytes 1769472 | tf_op jit(solution)/shard_map/all_gather | solution.py:52
  59.6 233.2 %all-reduce.3.cloned.1.call-start = ((), (), s32[]{:S(2)}) async-start(), calls=%async_computation.6 | async-start | bytes 2097152 | tf_op jit(solution)/shard_map/psum | solution.py:79
  59.6 164.0 %copy-start.13 = (pred[384]{0:T(512)(128)(4,1)}, pred[384]{0:T(512)(128)(4,1)S(1)}, u32[]{:S(2)}) copy-start(pred[384]{0:T(512)(128)(4,1)S(1)} %broadcast_compare_fusion.1) | copy-start | bytes 1156
  179.2 6.3 %copy-start.6 = (f32[4,128,128]{1,2,0:T(8,128)}, f32[4,128,128]{1,2,0:T(8,128)S(1)}, u32[]{:S(2)}) copy-start(f32[4,128,128]{1,2,0:T(8,128)S(1)} %custom-call.7) | copy-start | bytes 786436
  179.3 10.9 %slice-start.1 = ((s8[4718592]{0:T(1024)(128)(4,1)}), s8[4194304]{0:T(1024)(128)(4,1)S(1)}, s32[]{:S(2)}) async-start(s8[4718592]{0:T(1024)(128)(4,1)} %bitcast.99), calls=%async_computation.8 | async-start | bytes 8388608
  183.6 6.7 %slice-start.2 = ((s8[4718592]{0:T(1024)(128)(4,1)}), s8[524288]{0:T(1024)(128)(4,1)S(1)}, s32[]{:S(2)}) async-start(s8[4718592]{0:T(1024)(128)(4,1)} %bitcast.99), calls=%async_computation.9 | async-start | bytes 1048576
  197.4 164.1 %reduce-scatter.2.cloned.1.call-start = ((), (), s32[]{:S(2)}) async-start(), calls=%async_computation.5 | async-start | bytes 1769472 | tf_op jit(solution)/shard_map/reduce_scatter | solution.py:94
  202.0 1.5 copy-start.1
  222.4 7.5 %copy-start.11 = (f32[1152,384]{1,0:T(8,128)}, f32[1152,384]{1,0:T(8,128)S(1)}, u32[]{:S(2)}) copy-start(f32[1152,384]{1,0:T(8,128)S(1)} %fusion) | copy-start | bytes 5308420
  222.4 2.7 copy-start.5
  296.1 4.7 %copy-start.7 = (f32[4,128,128]{1,2,0:T(8,128)S(1)}, f32[4,128,128]{1,2,0:T(8,128)}, u32[]{:S(2)}) copy-start(f32[4,128,128]{1,2,0:T(8,128)} %copy-done.6) | copy-start | bytes 786436
  306.1 6.0 %copy-start.8 = (f32[512,128]{1,0:T(8,128)}, f32[512,128]{1,0:T(8,128)S(1)}, u32[]{:S(2)}) copy-start(f32[512,128]{1,0:T(8,128)S(1)} %copy.26) | copy-start | bytes 786436
  311.7 1.9 copy-start.9
  311.7 1.9 copy-start.10
  319.6 3.0 copy-start.2
  324.6 36.9 %copy-start.14 = (pred[384]{0:T(512)(128)(4,1)S(1)}, pred[384]{0:T(512)(128)(4,1)}, u32[]{:S(2)}) copy-start(pred[384]{0:T(512)(128)(4,1)} %copy-done.13) | copy-start | bytes 1156
  325.0 38.6 %copy-start.15 = (pred[256]{0:T(512)(128)(4,1)S(1)}, pred[256]{0:T(512)(128)(4,1)}, u32[]{:S(2)}) copy-start(pred[256]{0:T(512)(128)(4,1)} %compare_and_fusion) | copy-start | bytes 772
  327.1 36.5 %copy-start = (f32[1024,384]{1,0:T(8,128)S(1)}, f32[1024,384]{1,0:T(8,128)}, u32[]{:S(2)}) copy-start(f32[1024,384]{1,0:T(8,128)} %slice.173) | copy-start | bytes 4718596
Sparse Core Ops, SparseCore 0:
  12.3 40.1 all-gather.6
  54.5 74.6 all-gather.8
  130.7 35.6 all-gather.4
  168.3 44.4 all-gather.10
  216.2 76.5 all-reduce.2
  296.0 65.4 reduce-scatter.1
where the time goes:
time: 382 us; the launch traced here: 376 us
  waiting for transfers between devices  213 us (56%)
  other arithmetic  52.4 us (14%)
  matrix products  50.7 us (13%)
  local copies, waits for them, and re-layouts  45.4 us (12%)
  between operations  14.5 us (4%)
    all_gather x1, waiting for transfers between devices, local(): lax.all_gather(diag_part, 'row', axis=1, tiled=True)  68.9 us
    psum x1, waiting for transfers between devices, local(): diag_start = lax.psum(partial_sum, 'row')  61.6 us
    another operation x3, other arithmetic, local(): lax.linalg.triangular_solve(diag_block, adjoint_panels[:, first_row:botto...  41.2 us
    all_gather x1, waiting for transfers between devices, local(): lax.all_gather(factor_local, 'col', axis=2, tiled=True)  40.3 us
    reduce_scatter x1, waiting for transfers between devices, local(): lax.psum_scatter(row_terms, 'row', scatter_dimension=1, tiled=True)  34.3 us
    dot_general x8, matrix products, exact_dot(): jnp.dot(first, second, precision=lax.Precision.HIGHEST, preferred_element...  30.7 us
    another operation x7, matrix products, local(): lax.linalg.triangular_solve(diag_block, adjoint_panels[:, first_row:botto...  10.8 us
    unnamed x40, local copies, waits for them, and re-layouts  10.3 us
  transfers between devices with their start and end apart: 6, of which 5 were waited for; matrix products, arithmetic and copies ran while one was open for 34% of the time, Pallas kernels for 0%

commit v1 on v0

--- a/solution.py
+++ b/solution.py
@@ -50,7 +50,7 @@
     diag_part = factor_panels[:owned_rows].reshape(row_blocks, tile_rows, 2 * NB)
     top_rows, diag_full = (
         lax.all_gather(factor_tops, "row", axis=1, tiled=True),
-        lax.all_gather(diag_part, "row", axis=1, tiled=True),
+        jnp.concatenate(lax.all_gather(diag_part, "row"), axis=1),
     )
     top_rows = top_rows.reshape(2 * NB, local_cols)
     diag_full = diag_full.reshape(2 * NB, 2 * NB)

time: 382 us -> 381 us (level)
    unnamed x40 -> x30, local copies, waits for them, and re-layouts: 10.3 us -> 10.9 us
    another operation x20 -> x13, local copies, waits for them, and re-layouts: 8.75 us -> 9.28 us
  transfers between devices with their start and end apart: 6 -> 6, of which waited for: 5 -> 5; matrix products, arithmetic and copies ran while one was open for 34% -> 33% of each run, Pallas kernels for 0% -> 0%
where the time goes in v1:
time: 381 us; the launch traced here: 375 us
  waiting for transfers between devices  216 us (57%)
  other arithmetic  50.8 us (13%)
  matrix products  49.2 us (13%)
  local copies, waits for them, and re-layouts  43.9 us (12%)
  between operations  14.4 us (4%)
    all_gather x1, waiting for transfers between devices, local(): lax.all_gather(diag_part, 'row')  67.6 us
    psum x1, waiting for transfers between devices, local(): diag_start = lax.psum(partial_sum, 'row')  61.5 us
    another operation x3, other arithmetic, local(): lax.linalg.triangular_solve(diag_block, adjoint_panels[:, first_row:botto...  41.2 us
    all_gather x1, waiting for transfers between devices, local(): lax.all_gather(factor_local, 'col', axis=2, tiled=True)  40.3 us
    reduce_scatter x1, waiting for transfers between devices, local(): lax.psum_scatter(row_terms, 'row', scatter_dimension=1, tiled=True)  37.8 us
    dot_general x8, matrix products, exact_dot(): jnp.dot(first, second, precision=lax.Precision.HIGHEST, preferred_element...  30.7 us
    unnamed x30, local copies, waits for them, and re-layouts  10.9 us
    another operation x7, matrix products, local(): lax.linalg.triangular_solve(diag_block, adjoint_panels[:, first_row:botto...  10.9 us
  transfers between devices with their start and end apart: 6, of which 5 were waited for; matrix products, arithmetic and copies ran while one was open for 33% of the time, Pallas kernels for 0%

profile of v1, /device:TPU:0, one launch (start us, length us, event | category | flops | bytes accessed | tf_op | source)
XLA Modules:
  0.0 374.8 jit_solution(15651831652108530650)
XLA Ops:
  6.5 2.7 copy.53
  9.4 1.2 copy-done.4
  10.7 1.4 copy.72
  12.2 40.3 %all-gather.7.cloned.1.call-done = f32[1152,2,512]{0,2,1:T(8,128)} async-done(((f32[1152,2,128]{0,2,1:T(8,128)}), f32[1152,2,512]{0,2,1:T(8,128)}) %all-gather.7.cloned.1.call-update) | async-done | bytes 4718608 | tf_op jit(solution)/shard_map/all_gather | solution.py:46
  52.4 1.1 slice.166
  53.5 1.0 copy.73
  54.6 1.2 copy.51
  56.1 1.2 copy-done.3
  57.4 1.4 copy.71
  59.9 67.6 %all-gather.9.cloned.1.call-done = f32[8,1,128,1024]{3,2,1,0:T(8,128)} async-done(((f32[1,1,128,1024]{3,2,1,0:T(8,128)}), f32[8,1,128,1024]{3,2,1,0:T(8,128)}) %all-gather.9.cloned.1.call-update) | async-done | bytes 4194320 | tf_op jit(solution)/shard_map/all_gather | solution.py:53
  127.5 1.4 fusion.19
  128.9 8.4 %while.1 = (s32[]{:T(128)}, f32[512,512]{1,0:T(8,128)S(1)}, s32[4,2]{0,1:T(2,128)S(1)}, f32[4,128,128]{2,1,0:T(8,128)S(1)}, s32[]{:T(128)}) while((s32[]{:T(128)}, f32[512,512]{1,0:T(8,128)S(1)}, s32[4,2]{0,1:T(2,128)S(1)}, f32[4,128,128]{2,1,0:T(8,128)S(1)}, s32[]{:T(128)}) %tuple.22), condition=%wide.while_cond, body=%wide.while_body.sunk | while | flops 2 | bytes 131189 | solution.py:71
  129.5 1.4 bitcast_dynamic-update-slice_fusion.2
  131.6 1.4 bitcast_dynamic-update-slice_fusion.2
  133.7 1.4 bitcast_dynamic-update-slice_fusion.2
  135.8 1.4 bitcast_dynamic-update-slice_fusion.2
  137.2 39.8 %custom-call.7 = f32[4,128,128]{1,2,0:T(8,128)S(1)} custom-call(f32[4,128,128]{2,1,0:T(8,128)S(1)} %get-tuple-element.12), custom_call_target="InvertDiagBlocksLowerTriangular" | custom-call | tf_op jit(solution)/shard_map/triangular_solve | solution.py:71
  177.1 1.9 fusion.34
  179.0 1.7 convolution_subtract_fusion.2
  181.4 2.0 convolution_subtract_fusion.1
  184.1 2.5 convolution_subtract_fusion
  186.6 1.5 fusion.70
  188.1 4.4 %fusion.9 = f32[512,512]{1,0:T(8,128)S(1)} fusion(f32[1152,1024]{0,1:T(8,128)S(1)} %bitcast.101, pred[1152]{0:T(1024)(128)(4,1)S(1)} %broadcast_compare_fusion, f32[1152,128]{0,1:T(8,128)S(1)} %fusion.34, f32[1152,128]{0,1:T(8,128)S(1)} %fusion.64, f32[1152,128]{0,1:T(8,128)S(1)} %fusion.67, f32[1152,128]{0,1:T(8,128)S(1)} %fusion.70), kind=kOutput, calls=%fused_computation.29 | convolution fusion | flops 3627352064 | bytes 5771264 | tf_op jit(solution)/shard_map/dot_general | solution.py:10
  192.5 2.6 convolution_subtract_fusion.3
  195.3 4.3 %fusion.103 = (f32[1152,512]{0,1:T(8,128)}, f32[1152,512]{0,1:T(8,128)S(1)}) fusion(f32[1152,1024]{0,1:T(8,128)} %bitcast.86, f32[1152,128]{0,1:T(8,128)S(1)} %fusion.34, f32[1152,128]{0,1:T(8,128)S(1)} %fusion.64, f32[1152,128]{0,1:T(8,128)S(1)} %fusion.67, f32[1152,128]{0,1:T(8,128)S(1)} %fusion.70, pred[1152]{0:T(1024)(128)(4,1)S(1)} %broadcast_compare_fusion), kind=kLoop, calls=%fused_computation.162 | loop fusion | flops 2949120 | bytes 11797632 | tf_op jit(solution)/shard_map/slice | solution.py:107
  199.6 1.5 copy-done.1
  201.1 1.6 slice.177
  202.7 8.9 %all-gather.11.cloned.1.call-done = f32[1,1024,384]{1,2,0:T(8,128)} async-done(((f32[1,128,384]{1,2,0:T(8,128)}), f32[1,1024,384]{1,2,0:T(8,128)}) %all-gather.11.cloned.1.call-update) | async-done | bytes 1572880 | tf_op jit(solution)/shard_map/all_gather | solution.py:52
  211.7 9.6 %fusion = f32[1152,384]{1,0:T(8,128)S(1)} fusion(f32[1152,384]{1,0:T(8,128)} %copy-done.3, pred[384]{0:T(512)(128)(4,1)S(1)} %broadcast_compare_fusion.1, pred[1152]{0:T(1024)(128)(4,1)S(1)} %broadcast_compare_fusion, f32[1,1024,384]{1,2,0:T(8,128)} %all-gather.11.cloned.1.call-done, f32[1152,128]{0,1:T(8,128)S(1)} %fusion.34, f32[1152,128]{0,1:T(8,128)S(1)} %fusion.64, ...), kind=kOutput, calls=%fused_computation.6 | convolution fusion | flops 2721595392 | bytes 6689280 | tf_op jit(solution)/shard_map/dot_general | solution.py:10
  221.3 1.2 slice.173
  222.5 1.4 copy-done.5
  223.9 4.7 %fusion.2 = f32[512,384]{1,0:T(8,128)S(1)} fusion(f32[1152,384]{1,0:T(8,128)S(1)} %bitcast.91, pred[384]{0:T(512)(128)(4,1)S(1)} %broadcast_compare_fusion.1, pred[1152]{0:T(1024)(128)(4,1)S(1)} %broadcast_compare_fusion, f32[1152,128]{0,1:T(8,128)S(1)} %fusion.34, f32[1152,128]{0,1:T(8,128)S(1)} %fusion.64, f32[1152,128]{0,1:T(8,128)S(1)} %fusion.67, ...), kind=kOutput, calls=%fused_computation.15 | convolution fusion | flops 2721153024 | bytes 4916736 | tf_op jit(solution)/shard_map/dot_general | solution.py:10
  228.7 1.2 pad_bitcast_fusion
  230.0 61.5 %all-reduce.3.cloned.1.call-done = f32[512,512]{1,0:T(8,128)} async-done(((f32[512,512]{1,0:T(8,128)}), f32[512,512]{1,0:T(8,128)}) %all-reduce.3.cloned.1.call-update) | async-done | bytes 1048592 | tf_op jit(solution)/shard_map/psum | solution.py:79
  291.5 3.4 convolution_bitcast_fusion
  294.9 4.5 %gather_fusion = f32[512]{0:T(512)S(1)} fusion(f32[512,512]{1,0:T(8,128)S(1)} %convolution_bitcast_fusion, s32[512]{0:T(512)S(1)} %bitcast.79), kind=kCustom, calls=%fused_computation | custom fusion | bytes 8192 | tf_op jit(solution)/shard_map/jit(_diag)/jit(diagonal)/cond/branch_0_fun/gather | solution.py:16
  305.6 1.5 convolution_subtract_fusion.8
  308.5 1.2 bitcast_add_fusion.2
  309.7 4.8 %gather_fusion.1 = f32[512]{0:T(512)S(1)} fusion(f32[512,512]{1,0:T(8,128)S(1)} %bitcast_add_fusion.2, s32[512]{0:T(512)S(1)} %bitcast.80), kind=kCustom, calls=%fused_computation.1 | custom fusion | bytes 8192 | tf_op jit(solution)/shard_map/jit(_diag)/jit(diagonal)/cond/branch_0_fun/gather | solution.py:16
  314.7 1.3 copy.62
  316.0 2.0 convolution_select_fusion.1
  318.1 1.9 maximum_maximum_fusion
  320.4 1.8 fusion.18
  322.3 37.8 %reduce-scatter.2.cloned.1.call-done = f32[1,128,384]{2,1,0:T(8,128)} async-done(((f32[1,1024,384]{2,1,0:T(8,128)}), f32[1,128,384]{2,1,0:T(8,128)}) %reduce-scatter.2.cloned.1.call-update) | async-done | bytes 196624 | tf_op jit(solution)/shard_map/reduce_scatter | solution.py:94
  360.1 2.1 fusion.17
  362.3 1.3 fusion.3
  363.6 2.7 reshape.142
  366.3 1.4 copy.65
  (87 shorter events, 14.2 us)
Async XLA Ops:
  6.5 45.9 %all-gather.7.cloned.1.call-start = ((), (), s32[]{:S(2)}) async-start(), calls=%async_computation.2 | async-start | bytes 5898240 | tf_op jit(solution)/shard_map/all_gather | solution.py:46
  9.4 1.2 copy-start.4
  12.1 42.5 %copy-start.10 = (f32[9,128,3,128]{3,1,2,0:T(8,128)S(1)}, f32[9,128,3,128]{3,1,2,0:T(8,128)}, u32[]{:S(2)}) copy-start(f32[9,128,3,128]{3,1,2,0:T(8,128)} %param.3) | copy-start | bytes 5308420
  12.1 115.4 %all-gather.9.cloned.1.call-start = ((), (), s32[]{:S(2)}) async-start(), calls=%async_computation.3 | async-start | bytes 4718592 | tf_op jit(solution)/shard_map/all_gather | solution.py:53
  54.5 122.5 %all-gather.5.cloned.1.call-start = ((), (), s32[]{:S(2)}) async-start(), calls=%async_computation.1 | async-start | bytes 5898240 | tf_op jit(solution)/shard_map/all_gather | solution.py:66
  56.1 1.2 copy-start.3
  57.4 1.5 slice-start
  58.9 152.8 %all-gather.11.cloned.1.call-start = ((), (), s32[]{:S(2)}) async-start(), calls=%async_computation.4 | async-start | bytes 1769472 | tf_op jit(solution)/shard_map/all_gather | solution.py:52
  59.8 231.7 %all-reduce.3.cloned.1.call-start = ((), (), s32[]{:S(2)}) async-start(), calls=%async_computation.6 | async-start | bytes 2097152 | tf_op jit(solution)/shard_map/psum | solution.py:79
  177.1 6.3 %copy-start.6 = (f32[4,128,128]{1,2,0:T(8,128)}, f32[4,128,128]{1,2,0:T(8,128)S(1)}, u32[]{:S(2)}) copy-start(f32[4,128,128]{1,2,0:T(8,128)S(1)} %custom-call.7) | copy-start | bytes 786436
  177.1 11.0 %slice-start.1 = ((s8[4718592]{0:T(1024)(128)(4,1)}), s8[4194304]{0:T(1024)(128)(4,1)S(1)}, s32[]{:S(2)}) async-start(s8[4718592]{0:T(1024)(128)(4,1)} %bitcast.99), calls=%async_computation.8 | async-start | bytes 8388608
  181.4 6.7 %slice-start.2 = ((s8[4718592]{0:T(1024)(128)(4,1)}), s8[524288]{0:T(1024)(128)(4,1)S(1)}, s32[]{:S(2)}) async-start(s8[4718592]{0:T(1024)(128)(4,1)} %bitcast.99), calls=%async_computation.9 | async-start | bytes 1048576
  195.1 164.9 %reduce-scatter.2.cloned.1.call-start = ((), (), s32[]{:S(2)}) async-start(), calls=%async_computation.5 | async-start | bytes 1769472 | tf_op jit(solution)/shard_map/reduce_scatter | solution.py:94
  199.6 1.5 copy-start.1
  221.2 7.4 %copy-start.9 = (f32[1152,384]{1,0:T(8,128)}, f32[1152,384]{1,0:T(8,128)S(1)}, u32[]{:S(2)}) copy-start(f32[1152,384]{1,0:T(8,128)S(1)} %fusion) | copy-start | bytes 5308420
  221.3 2.7 copy-start.5
  294.9 4.7 %copy-start.7 = (f32[4,128,128]{1,2,0:T(8,128)S(1)}, f32[4,128,128]{1,2,0:T(8,128)}, u32[]{:S(2)}) copy-start(f32[4,128,128]{1,2,0:T(8,128)} %copy-done.6) | copy-start | bytes 786436
  307.4 0.7 copy-start.8
  314.7 3.4 copy-start.2
  322.3 39.9 %copy-start = (f32[1024,384]{1,0:T(8,128)S(1)}, f32[1024,384]{1,0:T(8,128)}, u32[]{:S(2)}) copy-start(f32[1024,384]{1,0:T(8,128)} %slice.173) | copy-start | bytes 4718596
Sparse Core Ops, SparseCore 0:
  12.2 40.1 all-gather.6
  54.7 72.7 all-gather.8
  129.1 36.0 all-gather.4
  167.1 44.5 all-gather.10
  215.0 76.4 all-reduce.2
  294.8 65.2 reduce-scatter.1
